TPU v7x, 768 devices: a whole 4x8x12 slice. The times are simulated.
768 devices in a mesh: seq: 96 (over y_hi, z, core), tp: 8 (over y_lo, x).
Axes of the slice: x: 4, y: 8 (y_hi: 4, y_lo: 2; y = y_hi * 2 + y_lo), z: 12, core: 2. Of those that a mesh axis runs over, the one named last changes fastest.
Arguments:
- queries: bfloat16 [98304, 4096], P(('seq', 'tp')), may hold values from -170 to 170, as said below
- keys: bfloat16 [98304, 512], P(('seq', 'tp')), may hold values from -6 to 6
- values: bfloat16 [98304, 512], P(('seq', 'tp')), may hold values from -6 to 6
- segments: int32 [98304], replicated, may hold values from 0 to 767, never falling along the last dimension, each value on 1 to 256 neighbouring positions
- out_weight: bfloat16 [4096, 4096], P('tp'), may hold values from -0.75 to 0.75
Outputs:
- mixed: bfloat16 [98304, 4096], P(('seq', 'tp'))
Inputs may be any that keep to these rules, and one draw needn't show every extreme that they name: `segments`: document ids never fall along the positions; one document holds at most 256 positions. `queries`: independent entries.
All inputs are finite; a program needn't handle non-finite values.
Results may differ from a plain program's by a relative error of at most 0.014.
Values may be sent and summed in bfloat16 or wider, within the bound.
No kernel may reach another device: no remote copies, remote signals or barrier semaphores. Data moves between devices by JAX's collectives and lax.ppermute only.
A program may use at most 64 MiB of HBM per device.

v0:
```python
import jax
import jax.numpy as jnp
from jax import lax
from jax.sharding import PartitionSpec as P

KVH = 4
HD = 128
DOC = 256


def from_behind(value, axis, steps):
    count = lax.axis_size(axis)
    first, last = (max(0, -steps), min(count, count - steps))
    return lax.ppermute(value, axis, [(source, source + steps) for source in range(first, last)])


def spread_heads(source, copies):
    rows = source.shape[0]
    widened = jnp.repeat(source.reshape(rows, KVH, HD), copies, axis=1)
    return widened.reshape(rows, KVH * copies * HD)


def shards(queries, keys, values, segments, out_weight):
    tp_count = lax.axis_size("tp")
    copies = max(tp_count // KVH, 1)
    tile_rows = DOC // 2
    inverse_root = HD ** (-0.5)
    keys_wide = spread_heads(keys, copies)
    values_wide = spread_heads(values, copies)
    local_queries, local_keys, local_values = (
        lax.all_to_all(queries, "tp", split_axis=1, concat_axis=0, tiled=True),
        lax.all_to_all(keys_wide, "tp", split_axis=1, concat_axis=0, tiled=True),
        lax.all_to_all(values_wide, "tp", split_axis=1, concat_axis=0, tiled=True),
    )
    row_count = local_queries.shape[0]
    kv_local = local_keys.shape[1] // HD
    query_local = local_queries.shape[1] // HD
    local_group = query_local // kv_local
    tile_count = row_count // tile_rows
    first_row = lax.axis_index("seq") * row_count
    closing = jnp.stack([local_keys[row_count - DOC :], local_values[row_count - DOC :]])
    earlier = from_behind(closing, "seq", 1)
    key_ext = jnp.concatenate([earlier[0], local_keys], 0).reshape(row_count + DOC, kv_local, HD)
    value_ext = jnp.concatenate([earlier[1], local_values], 0).reshape(
        row_count + DOC, kv_local, HD
    )
    padded_seg = jnp.concatenate([jnp.full((DOC,), -1, jnp.int32), segments], 0)
    key_seg = lax.dynamic_slice_in_dim(padded_seg, first_row, row_count + DOC)
    query_seg = key_seg[DOC:].reshape(tile_count, tile_rows)
    key_pos = first_row - DOC + jnp.arange(row_count + DOC, dtype=jnp.int32)
    query_pos = (first_row + jnp.arange(row_count, dtype=jnp.int32)).reshape(tile_count, tile_rows)

    def windows(source):
        blocks = source.reshape((tile_count + 2, tile_rows) + source.shape[1:])
        return jnp.concatenate([blocks[:-2], blocks[1:-1], blocks[2:]], 1)

    key_win = windows(key_ext)
    value_win = windows(value_ext)
    pos_win = windows(key_pos)
    seg_win = windows(key_seg)
    query_tiles = local_queries.reshape(tile_count, tile_rows, kv_local, local_group, HD)
    allowed = (pos_win[:, None, :] <= query_pos[:, :, None]) & (
        seg_win[:, None, :] == query_seg[:, :, None]
    )
    allowed = allowed[:, None, None]
    scores = (
        jnp.einsum("ctkgd,cskd->ckgts", query_tiles, key_win, preferred_element_type=jnp.float32)
        * inverse_root
    )
    masked = jnp.where(allowed, scores, jnp.float32(-1e30))
    top_score = jnp.max(masked, axis=-1, keepdims=True)
    weights = jnp.where(allowed, jnp.exp(masked - top_score), jnp.float32(0.0))
    denominator = jnp.sum(weights, axis=-1)
    totals = jnp.einsum(
        "ckgts,cskd->ckgtd",
        weights.astype(jnp.bfloat16),
        value_win,
        preferred_element_type=jnp.float32,
    )
    attended = (totals / denominator[..., None]).astype(jnp.bfloat16)
    attended = jnp.transpose(attended, (0, 3, 1, 2, 4)).reshape(row_count, query_local * HD)
    return lax.psum_scatter(
        jnp.dot(attended, out_weight, preferred_element_type=jnp.float32).astype(jnp.bfloat16),
        "tp",
        scatter_dimension=0,
        tiled=True,
    )


def solution(mesh):
    placed = (
        P(("seq", "tp"), None),
        P(("seq", "tp"), None),
        P(("seq", "tp"), None),
        P(),
        P("tp", None),
    )
    return jax.shard_map(
        shards, mesh=mesh, in_specs=placed, out_specs=P(("seq", "tp"), None), check_vma=False
    )
```

profile of v0, /device:TPU:1, one launch (start us, length us, event | category | flops | bytes accessed | tf_op | source)
XLA Modules:
  0.0 176.2 jit_solution(6101591689099130751)
XLA Ops:
  6.5 0.9 copy-done
  7.5 0.7 broadcast_in_dim.31
  8.2 5.9 %all-to-all-start = ((bf16[128,8,128]{2,0,1:T(8,128)(2,1)}), bf16[128,8,128]{2,0,1:T(8,128)(2,1)S(1)}, u32[]{:S(2)}, u32[]{:S(2)}) async-start(bf16[128,8,128]{2,0,1:T(8,128)(2,1)} %bitcast.3), calls=%async_computation | async-start | bytes 524288 | tf_op jit(solution)/shard_map/all_to_all | solution.py:32
  14.1 0.9 copy_bitcast_fusion
  15.0 5.1 %all-to-all-done = bf16[128,8,128]{2,0,1:T(8,128)(2,1)S(1)} async-done(((bf16[128,8,128]{2,0,1:T(8,128)(2,1)}), bf16[128,8,128]{2,0,1:T(8,128)(2,1)S(1)}, u32[]{:S(2)}, u32[]{:S(2)}) %all-to-all-start) | async-done | bytes 262176 | tf_op jit(solution)/shard_map/all_to_all | solution.py:32
  20.1 0.7 broadcast_in_dim.32
  20.9 3.4 %all-to-all-start.1 = ((bf16[128,8,128]{2,0,1:T(8,128)(2,1)}), bf16[128,8,128]{2,0,1:T(8,128)(2,1)S(1)}, u32[]{:S(2)}, u32[]{:S(2)}) async-start(bf16[128,8,128]{2,0,1:T(8,128)(2,1)} %bitcast.6), calls=%async_computation.1 | async-start | bytes 524288 | tf_op jit(solution)/shard_map/all_to_all | solution.py:33
  24.3 2.3 %copy.11 = bf16[128,4096]{0,1:T(8,128)(2,1)} copy(bf16[128,4096]{1,0:T(8,128)(2,1)} %param.5) | data formatting | bytes 2097152 | tf_op args[0]
  26.5 3.7 %all-to-all-done.1 = bf16[128,8,128]{2,0,1:T(8,128)(2,1)S(1)} async-done(((bf16[128,8,128]{2,0,1:T(8,128)(2,1)}), bf16[128,8,128]{2,0,1:T(8,128)(2,1)S(1)}, u32[]{:S(2)}, u32[]{:S(2)}) %all-to-all-start.1) | async-done | bytes 262176 | tf_op jit(solution)/shard_map/all_to_all | solution.py:33
  30.3 3.6 %all-to-all-start.2 = ((bf16[128,8,512]{0,2,1:T(8,128)(2,1)}), bf16[128,8,512]{0,2,1:T(8,128)(2,1)S(1)}, u32[]{:S(2)}, u32[]{:S(2)}) async-start(bf16[128,8,512]{0,2,1:T(8,128)(2,1)} %bitcast.17), calls=%async_computation.2 | async-start | bytes 2097152 | tf_op jit(solution)/shard_map/all_to_all | solution.py:31
  33.9 0.0 reduce-scatter.2.cloned.1.call-start
  34.0 0.1 fusion.24
  34.1 7.1 %collective-permute-start = (bf16[2,256,128]{2,1,0:T(8,128)(2,1)S(1)}, bf16[2,256,128]{2,1,0:T(8,128)(2,1)S(1)}, u32[]{:S(2)}, u32[]{:S(2)}) collective-permute-start(bf16[2,256,128]{2,1,0:T(8,128)(2,1)S(1)} %pad_maximum_fusion.2), channel_id=1, source_target_pairs={{0,8},{8,16},{16,24},{24,32},{32,40},{40,48},{48,56},{56,64},{64,7... | collective-permute-start | bytes 393224 | tf_op jit(solution)/shard_map/ppermute | solution.py:14
  41.3 1.2 compare_and_fusion
  42.4 7.0 %collective-permute-done = bf16[2,256,128]{2,1,0:T(8,128)(2,1)S(1)} collective-permute-done((bf16[2,256,128]{2,1,0:T(8,128)(2,1)S(1)}, bf16[2,256,128]{2,1,0:T(8,128)(2,1)S(1)}, u32[]{:S(2)}, u32[]{:S(2)}) %collective-permute-start) | collective-permute-done | bytes 131104 | tf_op jit(solution)/shard_map/ppermute | solution.py:14
  49.5 0.1 fusion.21
  49.6 0.0 all-to-all-done.2
  49.6 1.0 fusion
  50.6 1.7 fusion.1
  52.3 2.5 %fusion.9 = bf16[8,128,1,4,128]{4,1,3,0,2:T(8,128)(2,1)S(1)} fusion(f32[8,4,128]{2,1,0:T(4,128)S(1)} %fusion.1, f32[8,384,128,4]{2,1,3,0:T(8,128)S(1)} %get-tuple-element.18, f32[8,4,128]{2,1,0:T(4,128)S(1)} %get-tuple-element.17, pred[8,128,384]{1,2,0:T(8,128)(4,1)S(1)} %compare_and_fusion, bf16[8,128,1,128]{3,1,0,2:T(8,128)(2,1)S(1)} %bitcast.96, ...), kind=kOutput, calls=%fused_computation.13 | convolution fusion | flops 413925376 | bytes 8552448 | tf_op jit(solution)/shard_map/ckgts,cskd->ckgtd/dot_general | solution.py:74
  54.8 0.7 copy.14
  55.5 9.0 %convolution_convert_fusion = bf16[1024,4096]{1,0:T(8,128)(2,1)} fusion(bf16[512,4096]{1,0:T(8,128)(2,1)} %param.9, bf16[64,8,8,128]{3,2,1,0:T(8,128)(2,1)S(1)} %bitcast.98), kind=kOutput, calls=%fused_computation | convolution fusion | flops 4299161600 | bytes 13631488 | tf_op jit(solution)/shard_map/dot_general | solution.py:83
  64.6 0.0 reduce-scatter.2.cloned.1.call-update
  64.6 104.8 %reduce-scatter.2.cloned.1.call-done = bf16[128,4096]{1,0:T(8,128)(2,1)} async-done(((bf16[1024,4096]{1,0:T(8,128)(2,1)}), bf16[128,4096]{1,0:T(8,128)(2,1)}) %reduce-scatter.2.cloned.1.call-update) | async-done | bytes 1048592 | tf_op jit(solution)/shard_map/reduce_scatter | solution.py:82
  (12 shorter events, 0.1 us)
Async XLA Ops:
  6.5 0.9 copy-start
  6.5 27.4 %copy-start.1 = (s32[98304]{0:T(1024)S(1)}, s32[98304]{0:T(1024)}, u32[]{:S(2)}) copy-start(s32[98304]{0:T(1024)} %param.8) | copy-start | bytes 1179652
  8.2 11.9 %all-to-all-start = ((bf16[128,8,128]{2,0,1:T(8,128)(2,1)}), bf16[128,8,128]{2,0,1:T(8,128)(2,1)S(1)}, u32[]{:S(2)}, u32[]{:S(2)}) async-start(bf16[128,8,128]{2,0,1:T(8,128)(2,1)} %bitcast.3), calls=%async_computation | async-start | bytes 524288 | tf_op jit(solution)/shard_map/all_to_all | solution.py:32
  20.9 9.4 %all-to-all-start.1 = ((bf16[128,8,128]{2,0,1:T(8,128)(2,1)}), bf16[128,8,128]{2,0,1:T(8,128)(2,1)S(1)}, u32[]{:S(2)}, u32[]{:S(2)}) async-start(bf16[128,8,128]{2,0,1:T(8,128)(2,1)} %bitcast.6), calls=%async_computation.1 | async-start | bytes 524288 | tf_op jit(solution)/shard_map/all_to_all | solution.py:33
  30.3 19.3 %all-to-all-start.2 = ((bf16[128,8,512]{0,2,1:T(8,128)(2,1)}), bf16[128,8,512]{0,2,1:T(8,128)(2,1)S(1)}, u32[]{:S(2)}, u32[]{:S(2)}) async-start(bf16[128,8,512]{0,2,1:T(8,128)(2,1)} %bitcast.17), calls=%async_computation.2 | async-start | bytes 2097152 | tf_op jit(solution)/shard_map/all_to_all | solution.py:31
  33.9 135.5 %reduce-scatter.2.cloned.1.call-start = ((), (), s32[]{:S(2)}) async-start(), calls=%async_computation.4 | async-start | bytes 9437184 | tf_op jit(solution)/shard_map/reduce_scatter | solution.py:82
  34.1 15.3 %collective-permute-start = (bf16[2,256,128]{2,1,0:T(8,128)(2,1)S(1)}, bf16[2,256,128]{2,1,0:T(8,128)(2,1)S(1)}, u32[]{:S(2)}, u32[]{:S(2)}) collective-permute-start(bf16[2,256,128]{2,1,0:T(8,128)(2,1)S(1)} %pad_maximum_fusion.2), channel_id=1, source_target_pairs={{0,8},{8,16},{16,24},{24,32},{32,40},{40,48},{48,56},{56,64},{64,7... | collective-permute-start | bytes 393224 | tf_op jit(solution)/shard_map/ppermute | solution.py:14
Sparse Core Ops, SparseCore 0:
  64.7 104.6 reduce-scatter.1
where the time goes:
time: 177 us; the launch traced here: 176 us
  waiting for transfers between devices  121 us (68%)
  starting transfers between devices  20 us (11%)
  between operations  13.5 us (8%)
  matrix products  12.5 us (7%)
  local copies, waits for them, and re-layouts  6.43 us (4%)
  other arithmetic  3.04 us (2%)
    reduce_scatter x1, waiting for transfers between devices, shards(): lax.psum_scatter(jnp.dot(attended, out_weight, preferred_element_type=jnp...  105 us
    dot_general x1, matrix products, shards(): jnp.dot(attended, out_weight, preferred_element_type=jnp.float32)  9.02 us
    ppermute x1, starting transfers between devices, from_behind(): lax.ppermute(value, axis, [(source, source + steps) for source in range(f...  7.14 us
    ppermute x1, waiting for transfers between devices, from_behind(): lax.ppermute(value, axis, [(source, source + steps) for source in range(f...  7.02 us
    all_to_all x1, starting transfers between devices, shards(): lax.all_to_all(keys_wide, 'tp', split_axis=1, concat_axis=0, tiled=True)  5.85 us
    all_to_all x1, waiting for transfers between devices, shards(): lax.all_to_all(keys_wide, 'tp', split_axis=1, concat_axis=0, tiled=True)  5.15 us
    all_to_all x1, waiting for transfers between devices, shards(): lax.all_to_all(values_wide, 'tp', split_axis=1, concat_axis=0, tiled=True)  3.74 us
    all_to_all x1, starting transfers between devices, shards(): lax.all_to_all(queries, 'tp', split_axis=1, concat_axis=0, tiled=True)  3.56 us
  transfers between devices with their start and end apart: 5, of which 4 were waited for; matrix products, arithmetic and copies ran while one was open for 3% of the time, Pallas kernels for 0%

commit v1 on v0

v1 whole, which is shorter than its diff:
```python
import jax
import jax.numpy as jnp
from jax import lax
from jax.experimental import pallas as pl
from jax.experimental.pallas import tpu as pltpu
from jax.sharding import PartitionSpec as P


HD = 128
XN = 4
YN = 8
ZN = 12
CN = 2
B = 128
KV = 4 * HD
NEG = -1e30
LOG2E = 1.4426950408889634


def device_of(x, y, z, c):
    x, y, z = x % XN, y % YN, z % ZN
    return ((y // 2) * ZN * CN + z * CN + c) * 8 + (y % 2) * XN + x


def pairs_of(move):
    found = []
    for x in range(XN):
        for y in range(YN):
            for z in range(ZN):
                for c in range(CN):
                    found.append((device_of(x, y, z, c), device_of(*move(x, y, z, c))))
    return sorted(found)


def along_x(steps):
    return pairs_of(lambda x, y, z, c: (x + (steps if c == 0 else -steps), y, z, c))


def across_y():
    return pairs_of(lambda x, y, z, c: (x, y - 1 if c == 0 else y + 1, z, c))


def ends_to(steps):
    found = []
    for source, target in along_x(steps):
        if source % XN >= 2:
            found.append((source, target))
    return found


def across_cores():
    return pairs_of(lambda x, y, z, c: (x, y, z, 1 - c))


def next_row():
    rows = YN * ZN * CN
    return [(r * XN + x, (r + 1) * XN + x) for r in range(rows - 1) for x in (2, 3)]


def send(value, pairs):
    return lax.ppermute(value, ("seq", "tp"), pairs)


def vmem():
    return pl.BlockSpec(memory_space=pltpu.VMEM)


def smem():
    return pl.BlockSpec(memory_space=pltpu.SMEM)


def shape(rows, cols):
    return jax.ShapeDtypeStruct((rows, cols), jnp.bfloat16)


def kernel(body, out_shape, in_specs, flops=0, limit=8, **rest):
    many = isinstance(out_shape, list)
    return pl.pallas_call(
        body,
        out_shape=out_shape,
        in_specs=in_specs,
        out_specs=[vmem()] * len(out_shape) if many else vmem(),
        cost_estimate=pl.CostEstimate(
            flops=flops, bytes_accessed=1 << 20, transcendentals=0
        ),
        compiler_params=pltpu.CompilerParams(vmem_limit_bytes=limit << 20),
        **rest,
    )


def place(where, step):
    return (where[0] + XN + where[3] * step) % XN


def pack_body(where, q, k, v, raw, *outs):
    y, c = where[1], where[2]
    raw[:, 0:512] = k[...]
    raw[:, 512:1024] = v[...]
    for step in range(XN):
        d = place(where, step)
        out = outs[step]
        own = pl.multiple_of((2 * y + d // 2) * HD, HD)
        oth = pl.multiple_of((2 * (1 - y) + d // 2) * HD, HD)
        for at, (src, col) in enumerate(((k, own), (k, oth), (v, own), (v, oth))):
            out[:, at * HD : (at + 1) * HD] = src[:, pl.ds(col, HD)]
        a = pl.multiple_of((16 * y + 4 * d) * HD, 512)
        b = pl.multiple_of((16 * (1 - y) + 4 * d + 2 * c) * HD, 256)
        e = pl.multiple_of((16 * (1 - y) + 4 * d + 2 * (1 - c)) * HD, 256)
        out[:, KV : KV + 512] = q[:, pl.ds(a, 512)]
        out[:, KV + 512 : KV + 768] = q[:, pl.ds(b, 256)]
        out[:, KV + 768 : KV + 1024] = q[:, pl.ds(e, 256)]


def pack(where, queries, keys, values):
    return kernel(
        pack_body, [shape(B, 1024)] + [shape(B, KV + 1024)] * XN, [smem()] + [vmem()] * 3
    )(where, queries, keys, values)


def cut(where, weight):
    def body(where, weight, left, right, sems):
        row = pl.multiple_of(where[2] * 256, 256)
        copies = [
            pltpu.make_async_copy(
                weight.at[pl.ds(row, 256), pl.ds(first, cols)], out, sems.at[i]
            )
            for i, (first, cols, out) in enumerate(((0, LEFT, left), (LEFT, RIGHT, right)))
        ]
        for copy in copies:
            copy.start()
        for copy in copies:
            copy.wait()

    return kernel(
        body,
        [shape(256, LEFT), shape(256, RIGHT)],
        [smem(), pl.BlockSpec(memory_space=pltpu.HBM)],
        scratch_shapes=[pltpu.SemaphoreType.DMA((2,))],
    )(where, weight)


def pack_before(where, raw):
    def body(where, raw, *outs):
        for step in range(XN):
            d = place(where, step)
            own = 2 * where[1] + d // 2
            oth = 2 * (1 - where[1]) + d // 2
            for at, head in enumerate((own, oth, 4 + own, 4 + oth)):
                col = pl.multiple_of(head * HD, HD)
                outs[step][:, at * HD : (at + 1) * HD] = raw[:, pl.ds(col, HD)]

    return kernel(body, [shape(B, KV)] * XN, [smem(), vmem()])(where, raw)


def attend(where, seg, befores, packs, steps, weight=None):
    count = len(steps)
    load = weight is not None

    def body(where, seg, *refs):
        befores, packs, refs = refs[:XN], refs[XN : 2 * XN], refs[2 * XN :]
        if load:
            source, out, held, buf, sem = refs
            copy = pltpu.make_async_copy(source, held, sem)
            copy.start()
        else:
            out, buf = refs
        for step, ref in enumerate(befores):
            j = place(where, step)

            @pl.when(j >= 2)
            def _():
                buf[j - 2] = ref[...]

        for step, ref in enumerate(packs):
            buf[place(where, step) + 2] = ref[:, 0:KV]
        row = lax.broadcasted_iota(jnp.int32, (B, 3 * B), 0)
        col = lax.broadcasted_iota(jnp.int32, (B, 3 * B), 1)
        causal = (col - 2 * B) <= row
        for i, step in enumerate(steps):
            j = place(where, step)
            seen = []
            for w in range(3):
                at = where[4] + j + w - 2
                ids = jnp.where(at < 0, -1, seg[pl.ds(jnp.maximum(at, 0), 1), :])
                seen.append(jnp.broadcast_to(ids.astype(jnp.float32), (B, B)))
            own_seg = seen[2].T
            same = jnp.concatenate([own_seg - s for s in seen], axis=1) == 0.0
            bias = jnp.where(causal & same, 0.0, NEG)
            bias = jnp.concatenate([bias] * 4, axis=0)
            rows = slice(i * B, (i + 1) * B)
            for g in range(2):
                first = [KV + (g * 4 + h) * HD for h in range(4)]
                qh = jnp.concatenate([packs[step][:, f : f + HD] for f in first], axis=0)
                kh = buf[pl.ds(j, 3), :, g * HD : (g + 1) * HD].reshape(3 * B, HD)
                vh = buf[pl.ds(j, 3), :, (2 + g) * HD : (3 + g) * HD].reshape(3 * B, HD)
                s = lax.dot_general(
                    qh, kh, (((1,), (1,)), ((), ())), preferred_element_type=jnp.float32
                )
                s = s * (LOG2E * HD**-0.5) + bias
                top = jnp.max(s, axis=1, keepdims=True)
                w = jnp.exp2(s - top)
                den = jnp.sum(w, axis=1, keepdims=True)
                o = jnp.dot(w.astype(jnp.bfloat16), vh, preferred_element_type=jnp.float32)
                o = (o / den).astype(jnp.bfloat16)
                for h in range(4):
                    out[rows, (g * 4 + h) * HD : (g * 4 + h + 1) * HD] = o[h * B : (h + 1) * B]
        if load:
            copy.wait()

    scratch = [pltpu.VMEM((6, B, KV), jnp.bfloat16)]
    out_shape = shape(count * B, 1024)
    in_specs = [smem()] + [vmem()] * (1 + 2 * XN)
    operands = [where, seg, *befores, *packs]
    if load:
        scratch.append(pltpu.SemaphoreType.DMA(()))
        out_shape = [out_shape, shape(*weight.shape)]
        in_specs.append(pl.BlockSpec(memory_space=pltpu.HBM))
        operands.append(weight)
    return kernel(
        body, out_shape, in_specs, flops=count * 800000000, limit=8, scratch_shapes=scratch
    )(*operands)


def project(att, w_own, w_mine, w_other, first, cols):
    tile = 256
    blocks = att.shape[0] // B

    def body(att, own, mine, other, *outs):
        for t in range(cols // tile):
            here = slice(t * tile, (t + 1) * tile)
            src = slice(first + t * tile, first + (t + 1) * tile)
            acc = jnp.dot(att[:, 0:512], own[:, src], preferred_element_type=jnp.float32)
            acc += jnp.dot(att[:, 512:768], mine[:, here], preferred_element_type=jnp.float32)
            acc += jnp.dot(att[:, 768:1024], other[:, here], preferred_element_type=jnp.float32)
            acc = acc.astype(jnp.bfloat16)
            for k in range(blocks):
                outs[k][:, here] = acc[k * B : (k + 1) * B]

    return kernel(
        body, [shape(B, cols)] * blocks, [vmem()] * 4, flops=2 * blocks * B * 1024 * cols, limit=6
    )(att, w_own, w_mine, w_other)


def joined_of(own, arrived):
    def body(a, b, out):
        total = a[...].astype(jnp.float32) + b[...].astype(jnp.float32)
        out[...] = total.astype(jnp.bfloat16)

    return kernel(body, shape(*own.shape), [vmem()] * 2)(own, near(arrived))


def finish(parts_l, parts_r):
    def body(*refs):
        out = refs[4]
        for at, (first, cols) in enumerate(((0, LEFT), (LEFT, RIGHT))):
            a, b = (refs[at * 2 + i][...].astype(jnp.float32) for i in range(2))
            out[:, first : first + cols] = (a + b).astype(jnp.bfloat16)

    return kernel(body, shape(B, LEFT + RIGHT), [vmem()] * 4)(*parts_l, *parts_r)


def apart(value):
    return pltpu.with_memory_space_constraint(value, pltpu.HBM)


def near(value):
    return pltpu.with_memory_space_constraint(value, pltpu.VMEM)


LEFT, RIGHT = 2560, 1536


def layer(queries, keys, values, segments, out_weight):
    seq = lax.axis_index("seq")
    tp = lax.axis_index("tp")
    x, y, c = tp % XN, tp // XN, seq % CN
    where = jnp.stack([x, y, c, 1 - 2 * c, seq * 8 + y * XN]).astype(jnp.int32)
    onward, back, far = along_x(1), along_x(-1), along_x(2)

    w_l, w_r = cut(where, apart(out_weight))
    raw, pack0, pack1, pack2, pack3 = pack(where, near(queries), near(keys), near(values))
    raw = near(send(raw, next_row()))
    packs = [
        near(pack0), near(send(pack3, back)), near(send(pack2, far)), near(send(pack1, onward))
    ]
    mine_l = near(send(w_l, across_y()))
    mine_r = near(send(w_r, across_y()))
    before0, before1, before2, before3 = pack_before(where, raw)
    befores = [
        near(before0),
        near(send(before3, ends_to(-1))),
        near(send(before2, ends_to(2))),
        near(send(before1, ends_to(1))),
    ]

    seg = near(segments.reshape(-1, B))

    other_l = near(send(mine_l, across_cores()))
    other_r = near(send(mine_r, across_cores()))

    att_a, w_own = attend(where, seg, befores, packs, (3,), apart(out_weight))
    w_own = near(w_own)
    (p3l,) = project(att_a, w_own, mine_l, other_l, 0, LEFT)
    l1 = send(p3l, onward)
    att_b = attend(where, seg, befores, packs, (2, 1, 0))
    (p3r,) = project(att_a, w_own, mine_r, other_r, LEFT, RIGHT)
    r1 = send(p3r, onward)
    p2l, p1l, p0l = project(att_b, w_own, mine_l, other_l, 0, LEFT)
    p2r, p1r, p0r = project(att_b, w_own, mine_r, other_r, LEFT, RIGHT)
    l2 = send(joined_of(p2l, l1), onward)
    r2 = send(joined_of(p2r, r1), onward)
    l3 = send(joined_of(p1l, l2), onward)
    r3 = send(joined_of(p1r, r2), onward)
    return finish([p0l, near(l3)], [p0r, near(r3)])


def solution(mesh):
    placed = (
        P(("seq", "tp"), None),
        P(("seq", "tp"), None),
        P(("seq", "tp"), None),
        P(),
        P("tp", None),
    )
    return jax.shard_map(
        layer, mesh=mesh, in_specs=placed, out_specs=P(("seq", "tp"), None), check_vma=False
    )
```

time: 177 us -> 137 us (0.77)
  the two profiles are of different devices: /device:TPU:1 before, /device:TPU:32 now
where the time goes in v1:
time: 137 us; the launch traced here: 136 us
  starting transfers between devices  61.6 us (45%)
  waiting for transfers between devices  58.1 us (42%)
  Pallas kernels  16.2 us (12%)
    ppermute x17, starting transfers between devices, send(): return lax.ppermute(value, ('seq', 'tp'), pairs)  61.6 us
    ppermute x17, waiting for transfers between devices, send(): return lax.ppermute(value, ('seq', 'tp'), pairs)  58.1 us
    pallas_call x2, Pallas kernels, attend(): kernel(body, out_shape, in_specs, flops=count * 800000000, limit=8, scrat...  5.76 us
    pallas_call x4, Pallas kernels, project(): kernel(body, [shape(B, cols)] * blocks, [vmem()] * 4, flops=2 * blocks *...  5.15 us
  transfers between devices with their start and end apart: 17, of which 7 were waited for; matrix products, arithmetic and copies ran while one was open for 0% of the time, Pallas kernels for 9%

profile of v1, /device:TPU:32, one launch (start us, length us, event | category | flops | bytes accessed | tf_op | source)
XLA Modules:
  0.0 136.3 jit_solution(12895776319339062631)
XLA Ops:
  0.1 2.1 %shard_map.59 = (bf16[256,2560]{1,0:T(8,128)(2,1)S(1)}, bf16[256,1536]{1,0:T(8,128)(2,1)S(1)}) custom-call(s32[5]{0:T(128)S(1)} %stack.23.where, bf16[512,4096]{1,0:T(8,128)(2,1)} %weight.1), custom_call_target="tpu_custom_call" | custom-call | bytes 1048576 | tf_op jit(solution)/shard_map/pallas_call | solution.py:134
  2.2 2.5 %collective-permute-start.7 = (bf16[256,2560]{1,0:T(8,128)(2,1)S(1)}, bf16[256,2560]{1,0:T(8,128)(2,1)S(1)}, u32[]{:S(2)}, u32[]{:S(2)}) collective-permute-start(bf16[256,2560]{1,0:T(8,128)(2,1)S(1)} %get-tuple-element.34), channel_id=1, source_target_pairs={{0,580},{1,581},{2,582},{3,583},{4,0},{5,1},{6,2},{7,3},{8,12},{9,... | collective-permute-start | bytes 3932168 | tf_op jit(solution)/shard_map/ppermute | solution.py:61
  4.7 17.1 %collective-permute-done.7.mine = bf16[256,2560]{1,0:T(8,128)(2,1)S(1)} collective-permute-done((bf16[256,2560]{1,0:T(8,128)(2,1)S(1)}, bf16[256,2560]{1,0:T(8,128)(2,1)S(1)}, u32[]{:S(2)}, u32[]{:S(2)}) %collective-permute-start.7) | collective-permute-done | bytes 1310752 | tf_op jit(solution)/shard_map/ppermute | solution.py:61
  21.8 1.9 %collective-permute-start.8 = (bf16[256,2560]{1,0:T(8,128)(2,1)S(1)}, bf16[256,2560]{1,0:T(8,128)(2,1)S(1)}, u32[]{:S(2)}, u32[]{:S(2)}) collective-permute-start(bf16[256,2560]{1,0:T(8,128)(2,1)S(1)} %collective-permute-done.7.mine), channel_id=1, source_target_pairs={{0,8},{1,9},{2,10},{3,11},{4,12},{5,13},{6,14},{7,15},{8,0},{9,1},... | collective-permute-start | bytes 3932168 | tf_op jit(solution)/shard_map/ppermute | solution.py:61
  25.2 3.6 %collective-permute-start.12 = (bf16[256,1536]{1,0:T(8,128)(2,1)S(1)}, bf16[256,1536]{1,0:T(8,128)(2,1)S(1)}, u32[]{:S(2)}, u32[]{:S(2)}) collective-permute-start(bf16[256,1536]{1,0:T(8,128)(2,1)S(1)} %get-tuple-element.39), channel_id=1, source_target_pairs={{0,580},{1,581},{2,582},{3,583},{4,0},{5,1},{6,2},{7,3},{8,12},{9,... | collective-permute-start | bytes 2359304 | tf_op jit(solution)/shard_map/ppermute | solution.py:61
  32.8 23.5 %collective-permute-start.4 = (bf16[128,1536]{1,0:T(8,128)(2,1)S(1)}, bf16[128,1536]{1,0:T(8,128)(2,1)S(1)}, u32[]{:S(2)}, u32[]{:S(2)}) collective-permute-start(bf16[128,1536]{1,0:T(8,128)(2,1)S(1)} %get-tuple-element.30), channel_id=1, source_target_pairs={{0,3},{1,0},{2,1},{3,2},{4,7},{5,4},{6,5},{7,6},{8,9},{9,10},{10,1... | collective-permute-start | bytes 1179656 | tf_op jit(solution)/shard_map/ppermute | solution.py:61
  56.4 8.3 %collective-permute-start.5 = (bf16[128,1536]{1,0:T(8,128)(2,1)S(1)}, bf16[128,1536]{1,0:T(8,128)(2,1)S(1)}, u32[]{:S(2)}, u32[]{:S(2)}) collective-permute-start(bf16[128,1536]{1,0:T(8,128)(2,1)S(1)} %get-tuple-element.31), channel_id=1, source_target_pairs={{0,2},{1,3},{2,0},{3,1},{4,6},{5,7},{6,4},{7,5},{8,10},{9,11},{10,... | collective-permute-start | bytes 1179656 | tf_op jit(solution)/shard_map/ppermute | solution.py:61
  64.7 1.9 %collective-permute-start.6 = (bf16[128,1536]{1,0:T(8,128)(2,1)S(1)}, bf16[128,1536]{1,0:T(8,128)(2,1)S(1)}, u32[]{:S(2)}, u32[]{:S(2)}) collective-permute-start(bf16[128,1536]{1,0:T(8,128)(2,1)S(1)} %get-tuple-element.32), channel_id=1, source_target_pairs={{0,1},{1,2},{2,3},{3,0},{4,5},{5,6},{6,7},{7,4},{8,11},{9,8},{10,9... | collective-permute-start | bytes 1179656 | tf_op jit(solution)/shard_map/ppermute | solution.py:61
  66.6 3.8 %collective-permute-done.5.refs_6_ = bf16[128,1536]{1,0:T(8,128)(2,1)S(1)} collective-permute-done((bf16[128,1536]{1,0:T(8,128)(2,1)S(1)}, bf16[128,1536]{1,0:T(8,128)(2,1)S(1)}, u32[]{:S(2)}, u32[]{:S(2)}) %collective-permute-start.5) | collective-permute-done | bytes 393248 | tf_op jit(solution)/shard_map/ppermute | solution.py:61
  70.4 5.2 %collective-permute-done.6.refs_7_ = bf16[128,1536]{1,0:T(8,128)(2,1)S(1)} collective-permute-done((bf16[128,1536]{1,0:T(8,128)(2,1)S(1)}, bf16[128,1536]{1,0:T(8,128)(2,1)S(1)}, u32[]{:S(2)}, u32[]{:S(2)}) %collective-permute-start.6) | collective-permute-done | bytes 393248 | tf_op jit(solution)/shard_map/ppermute | solution.py:61
  75.5 2.7 %shard_map.58 = (bf16[128,1024]{1,0:T(8,128)(2,1)S(1)}, bf16[512,4096]{1,0:T(8,128)(2,1)S(1)}) custom-call(s32[5]{0:T(128)S(1)} %stack.23.where, s32[768,128]{1,0:T(8,128)S(1)} %bitcast.6, bf16[128,512]{1,0:T(8,128)(2,1)S(1)} %get-tuple-element.25.refs_0_, bf16[128,512]{1,0:T(8,128)(2,1)S(1)} %collective-permute-done.1.refs_1_, ...), custom_call_target="tpu_custom_call" | custom-call | flops 800000000 | bytes 1048576 | tf_op jit(solution)/shard_map/pallas_call | solution.py:219
  78.3 1.9 %collective-permute-start.13 = (bf16[256,1536]{1,0:T(8,128)(2,1)S(1)}, bf16[256,1536]{1,0:T(8,128)(2,1)S(1)}, u32[]{:S(2)}, u32[]{:S(2)}) collective-permute-start(bf16[256,1536]{1,0:T(8,128)(2,1)S(1)} %collective-permute-done.12.mine), channel_id=1, source_target_pairs={{0,8},{1,9},{2,10},{3,11},{4,12},{5,13},{6,14},{7,15},{8,0},{9,1},... | collective-permute-start | bytes 2359304 | tf_op jit(solution)/shard_map/ppermute | solution.py:61
  81.1 3.0 %collective-permute-start.9 = (bf16[128,2560]{1,0:T(8,128)(2,1)S(1)}, bf16[128,2560]{1,0:T(8,128)(2,1)S(1)}, u32[]{:S(2)}, u32[]{:S(2)}) collective-permute-start(bf16[128,2560]{1,0:T(8,128)(2,1)S(1)} %shard_map.61), channel_id=1, source_target_pairs={{0,1},{1,2},{2,3},{3,0},{4,5},{5,6},{6,7},{7,4},{8,11},{9,8},{10,9... | collective-permute-start | bytes 1966088 | tf_op jit(solution)/shard_map/ppermute | solution.py:61
  84.2 3.0 %shard_map.57.att = bf16[384,1024]{1,0:T(8,128)(2,1)S(1)} custom-call(s32[5]{0:T(128)S(1)} %stack.23.where, s32[768,128]{1,0:T(8,128)S(1)} %bitcast.7, bf16[128,512]{1,0:T(8,128)(2,1)S(1)} %get-tuple-element.25.refs_0_, bf16[128,512]{1,0:T(8,128)(2,1)S(1)} %collective-permute-done.1.refs_1_, bf16[128,512]{1,0:T(8,128)(2,1)S(1)} %collective-permute-done.2.refs_2_, ...), custom_call_target="tpu_custom_call" | custom-call | flops 2400000000 | bytes 1048576 | tf_op jit(solution)/shard_map/pallas_call | solution.py:219
  87.2 2.2 %shard_map.60 = (bf16[128,2560]{1,0:T(8,128)(2,1)S(1)}, bf16[128,2560]{1,0:T(8,128)(2,1)S(1)}, bf16[128,2560]{1,0:T(8,128)(2,1)S(1)}) custom-call(bf16[384,1024]{1,0:T(8,128)(2,1)S(1)} %shard_map.57.att, bf16[512,4096]{1,0:T(8,128)(2,1)S(1)} %get-tuple-element.33.own, bf16[256,2560]{1,0:T(8,128)(2,1)S(1)} %collective-permute-done.7.mine, ...), custom_call_target="tpu_custom_call" | custom-call | flops 2013265920 | bytes 1048576 | tf_op jit(solution)/shard_map/pallas_call | solution.py:239
  89.5 5.4 %collective-permute-done.9.b = bf16[128,2560]{1,0:T(8,128)(2,1)S(1)} collective-permute-done((bf16[128,2560]{1,0:T(8,128)(2,1)S(1)}, bf16[128,2560]{1,0:T(8,128)(2,1)S(1)}, u32[]{:S(2)}, u32[]{:S(2)}) %collective-permute-start.9) | collective-permute-done | bytes 655392 | tf_op jit(solution)/shard_map/ppermute | solution.py:61
  95.0 1.9 %collective-permute-start.10 = (bf16[128,2560]{1,0:T(8,128)(2,1)S(1)}, bf16[128,2560]{1,0:T(8,128)(2,1)S(1)}, u32[]{:S(2)}, u32[]{:S(2)}) collective-permute-start(bf16[128,2560]{1,0:T(8,128)(2,1)S(1)} %shard_map.62), channel_id=1, source_target_pairs={{0,1},{1,2},{2,3},{3,0},{4,5},{5,6},{6,7},{7,4},{8,11},{9,8},{10,9... | collective-permute-start | bytes 1966088 | tf_op jit(solution)/shard_map/ppermute | solution.py:61
  97.6 3.2 %collective-permute-start.14 = (bf16[128,1536]{1,0:T(8,128)(2,1)S(1)}, bf16[128,1536]{1,0:T(8,128)(2,1)S(1)}, u32[]{:S(2)}, u32[]{:S(2)}) collective-permute-start(bf16[128,1536]{1,0:T(8,128)(2,1)S(1)} %shard_map.65), channel_id=1, source_target_pairs={{0,1},{1,2},{2,3},{3,0},{4,5},{5,6},{6,7},{7,4},{8,11},{9,8},{10,9... | collective-permute-start | bytes 1179656 | tf_op jit(solution)/shard_map/ppermute | solution.py:61
  102.2 10.7 %collective-permute-done.14.b = bf16[128,1536]{1,0:T(8,128)(2,1)S(1)} collective-permute-done((bf16[128,1536]{1,0:T(8,128)(2,1)S(1)}, bf16[128,1536]{1,0:T(8,128)(2,1)S(1)}, u32[]{:S(2)}, u32[]{:S(2)}) %collective-permute-start.14) | collective-permute-done | bytes 393248 | tf_op jit(solution)/shard_map/ppermute | solution.py:61
  113.0 1.9 %collective-permute-start.15 = (bf16[128,1536]{1,0:T(8,128)(2,1)S(1)}, bf16[128,1536]{1,0:T(8,128)(2,1)S(1)}, u32[]{:S(2)}, u32[]{:S(2)}) collective-permute-start(bf16[128,1536]{1,0:T(8,128)(2,1)S(1)} %shard_map.66), channel_id=1, source_target_pairs={{0,1},{1,2},{2,3},{3,0},{4,5},{5,6},{6,7},{7,4},{8,11},{9,8},{10,9... | collective-permute-start | bytes 1179656 | tf_op jit(solution)/shard_map/ppermute | solution.py:61
  115.1 2.0 %collective-permute-start.11 = (bf16[128,2560]{1,0:T(8,128)(2,1)S(1)}, bf16[128,2560]{1,0:T(8,128)(2,1)S(1)}, u32[]{:S(2)}, u32[]{:S(2)}) collective-permute-start(bf16[128,2560]{1,0:T(8,128)(2,1)S(1)} %shard_map.63), channel_id=1, source_target_pairs={{0,1},{1,2},{2,3},{3,0},{4,5},{5,6},{6,7},{7,4},{8,11},{9,8},{10,9... | collective-permute-start | bytes 1966088 | tf_op jit(solution)/shard_map/ppermute | solution.py:61
  117.1 6.8 %collective-permute-done.15.b = bf16[128,1536]{1,0:T(8,128)(2,1)S(1)} collective-permute-done((bf16[128,1536]{1,0:T(8,128)(2,1)S(1)}, bf16[128,1536]{1,0:T(8,128)(2,1)S(1)}, u32[]{:S(2)}, u32[]{:S(2)}) %collective-permute-start.15) | collective-permute-done | bytes 393248 | tf_op jit(solution)/shard_map/ppermute | solution.py:61
  124.0 1.9 %collective-permute-start.16 = (bf16[128,1536]{1,0:T(8,128)(2,1)S(1)}, bf16[128,1536]{1,0:T(8,128)(2,1)S(1)}, u32[]{:S(2)}, u32[]{:S(2)}) collective-permute-start(bf16[128,1536]{1,0:T(8,128)(2,1)S(1)} %shard_map.67), channel_id=1, source_target_pairs={{0,1},{1,2},{2,3},{3,0},{4,5},{5,6},{6,7},{7,4},{8,11},{9,8},{10,9... | collective-permute-start | bytes 1179656 | tf_op jit(solution)/shard_map/ppermute | solution.py:61
  125.9 9.2 %collective-permute-done.16.refs_3_ = bf16[128,1536]{1,0:T(8,128)(2,1)S(1)} collective-permute-done((bf16[128,1536]{1,0:T(8,128)(2,1)S(1)}, bf16[128,1536]{1,0:T(8,128)(2,1)S(1)}, u32[]{:S(2)}, u32[]{:S(2)}) %collective-permute-start.16) | collective-permute-done | bytes 393248 | tf_op jit(solution)/shard_map/ppermute | solution.py:61
  (33 shorter events, 10.1 us)
Async XLA Ops:
  0.1 23.7 %copy-start = (bf16[128,4096]{1,0:T(8,128)(2,1)S(1)}, bf16[128,4096]{1,0:T(8,128)(2,1)}, u32[]{:S(2)}) copy-start(bf16[128,4096]{1,0:T(8,128)(2,1)} %q.1) | copy-start | bytes 3145732
  0.1 23.7 %copy-start.2 = (bf16[128,512]{1,0:T(8,128)(2,1)S(1)}, bf16[128,512]{1,0:T(8,128)(2,1)}, u32[]{:S(2)}) copy-start(bf16[128,512]{1,0:T(8,128)(2,1)} %k.1) | copy-start | bytes 393220
  0.1 23.7 %copy-start.3 = (bf16[128,512]{1,0:T(8,128)(2,1)S(1)}, bf16[128,512]{1,0:T(8,128)(2,1)}, u32[]{:S(2)}) copy-start(bf16[128,512]{1,0:T(8,128)(2,1)} %v.1) | copy-start | bytes 393220
  2.2 73.4 %copy-start.1 = (s32[98304]{0:T(1024)S(1)}, s32[98304]{0:T(1024)}, u32[]{:S(2)}) copy-start(s32[98304]{0:T(1024)} %param.8) | copy-start | bytes 1179652
  2.2 19.6 %collective-permute-start.7 = (bf16[256,2560]{1,0:T(8,128)(2,1)S(1)}, bf16[256,2560]{1,0:T(8,128)(2,1)S(1)}, u32[]{:S(2)}, u32[]{:S(2)}) collective-permute-start(bf16[256,2560]{1,0:T(8,128)(2,1)S(1)} %get-tuple-element.34), channel_id=1, source_target_pairs={{0,580},{1,581},{2,582},{3,583},{4,0},{5,1},{6,2},{7,3},{8,12},{9,... | collective-permute-start | bytes 3932168 | tf_op jit(solution)/shard_map/ppermute | solution.py:61
  21.8 58.4 %collective-permute-start.8 = (bf16[256,2560]{1,0:T(8,128)(2,1)S(1)}, bf16[256,2560]{1,0:T(8,128)(2,1)S(1)}, u32[]{:S(2)}, u32[]{:S(2)}) collective-permute-start(bf16[256,2560]{1,0:T(8,128)(2,1)S(1)} %collective-permute-done.7.mine), channel_id=1, source_target_pairs={{0,8},{1,9},{2,10},{3,11},{4,12},{5,13},{6,14},{7,15},{8,0},{9,1},... | collective-permute-start | bytes 3932168 | tf_op jit(solution)/shard_map/ppermute | solution.py:61
  24.5 4.3 %collective-permute-start = (bf16[128,1024]{1,0:T(8,128)(2,1)S(1)}, bf16[128,1024]{1,0:T(8,128)(2,1)S(1)}, u32[]{:S(2)}, u32[]{:S(2)}) collective-permute-start(bf16[128,1024]{1,0:T(8,128)(2,1)S(1)} %get-tuple-element.24), channel_id=1, source_target_pairs={{2,6},{3,7},{6,10},{7,11},{10,14},{11,15},{14,18},{15,19},{18,22},... | collective-permute-start | bytes 786440 | tf_op jit(solution)/shard_map/ppermute | solution.py:61
  25.2 53.1 %collective-permute-start.12 = (bf16[256,1536]{1,0:T(8,128)(2,1)S(1)}, bf16[256,1536]{1,0:T(8,128)(2,1)S(1)}, u32[]{:S(2)}, u32[]{:S(2)}) collective-permute-start(bf16[256,1536]{1,0:T(8,128)(2,1)S(1)} %get-tuple-element.39), channel_id=1, source_target_pairs={{0,580},{1,581},{2,582},{3,583},{4,0},{5,1},{6,2},{7,3},{8,12},{9,... | collective-permute-start | bytes 2359304 | tf_op jit(solution)/shard_map/ppermute | solution.py:61
  29.5 3.3 %collective-permute-start.1 = (bf16[128,512]{1,0:T(8,128)(2,1)S(1)}, bf16[128,512]{1,0:T(8,128)(2,1)S(1)}, u32[]{:S(2)}, u32[]{:S(2)}) collective-permute-start(bf16[128,512]{1,0:T(8,128)(2,1)S(1)} %get-tuple-element.26), channel_id=1, source_target_pairs={{2,1},{3,2},{6,5},{7,6},{10,11},{11,8},{14,15},{15,12},{18,17},{19... | collective-permute-start | bytes 393224 | tf_op jit(solution)/shard_map/ppermute | solution.py:61
  30.2 26.2 %collective-permute-start.2 = (bf16[128,512]{1,0:T(8,128)(2,1)S(1)}, bf16[128,512]{1,0:T(8,128)(2,1)S(1)}, u32[]{:S(2)}, u32[]{:S(2)}) collective-permute-start(bf16[128,512]{1,0:T(8,128)(2,1)S(1)} %get-tuple-element.27), channel_id=1, source_target_pairs={{2,0},{3,1},{6,4},{7,5},{10,8},{11,9},{14,12},{15,13},{18,16},{19,... | collective-permute-start | bytes 393224 | tf_op jit(solution)/shard_map/ppermute | solution.py:61
  31.5 33.1 %collective-permute-start.3 = (bf16[128,512]{1,0:T(8,128)(2,1)S(1)}, bf16[128,512]{1,0:T(8,128)(2,1)S(1)}, u32[]{:S(2)}, u32[]{:S(2)}) collective-permute-start(bf16[128,512]{1,0:T(8,128)(2,1)S(1)} %get-tuple-element.28), channel_id=1, source_target_pairs={{2,3},{3,0},{6,7},{7,4},{10,9},{11,10},{14,13},{15,14},{18,19},{19... | collective-permute-start | bytes 393224 | tf_op jit(solution)/shard_map/ppermute | solution.py:61
  32.8 33.8 %collective-permute-start.4 = (bf16[128,1536]{1,0:T(8,128)(2,1)S(1)}, bf16[128,1536]{1,0:T(8,128)(2,1)S(1)}, u32[]{:S(2)}, u32[]{:S(2)}) collective-permute-start(bf16[128,1536]{1,0:T(8,128)(2,1)S(1)} %get-tuple-element.30), channel_id=1, source_target_pairs={{0,3},{1,0},{2,1},{3,2},{4,7},{5,4},{6,5},{7,6},{8,9},{9,10},{10,1... | collective-permute-start | bytes 1179656 | tf_op jit(solution)/shard_map/ppermute | solution.py:61
  56.4 14.0 %collective-permute-start.5 = (bf16[128,1536]{1,0:T(8,128)(2,1)S(1)}, bf16[128,1536]{1,0:T(8,128)(2,1)S(1)}, u32[]{:S(2)}, u32[]{:S(2)}) collective-permute-start(bf16[128,1536]{1,0:T(8,128)(2,1)S(1)} %get-tuple-element.31), channel_id=1, source_target_pairs={{0,2},{1,3},{2,0},{3,1},{4,6},{5,7},{6,4},{7,5},{8,10},{9,11},{10,... | collective-permute-start | bytes 1179656 | tf_op jit(solution)/shard_map/ppermute | solution.py:61
  64.7 10.9 %collective-permute-start.6 = (bf16[128,1536]{1,0:T(8,128)(2,1)S(1)}, bf16[128,1536]{1,0:T(8,128)(2,1)S(1)}, u32[]{:S(2)}, u32[]{:S(2)}) collective-permute-start(bf16[128,1536]{1,0:T(8,128)(2,1)S(1)} %get-tuple-element.32), channel_id=1, source_target_pairs={{0,1},{1,2},{2,3},{3,0},{4,5},{5,6},{6,7},{7,4},{8,11},{9,8},{10,9... | collective-permute-start | bytes 1179656 | tf_op jit(solution)/shard_map/ppermute | solution.py:61
  78.3 18.6 %collective-permute-start.13 = (bf16[256,1536]{1,0:T(8,128)(2,1)S(1)}, bf16[256,1536]{1,0:T(8,128)(2,1)S(1)}, u32[]{:S(2)}, u32[]{:S(2)}) collective-permute-start(bf16[256,1536]{1,0:T(8,128)(2,1)S(1)} %collective-permute-done.12.mine), channel_id=1, source_target_pairs={{0,8},{1,9},{2,10},{3,11},{4,12},{5,13},{6,14},{7,15},{8,0},{9,1},... | collective-permute-start | bytes 2359304 | tf_op jit(solution)/shard_map/ppermute | solution.py:61
  81.1 13.7 %collective-permute-start.9 = (bf16[128,2560]{1,0:T(8,128)(2,1)S(1)}, bf16[128,2560]{1,0:T(8,128)(2,1)S(1)}, u32[]{:S(2)}, u32[]{:S(2)}) collective-permute-start(bf16[128,2560]{1,0:T(8,128)(2,1)S(1)} %shard_map.61), channel_id=1, source_target_pairs={{0,1},{1,2},{2,3},{3,0},{4,5},{5,6},{6,7},{7,4},{8,11},{9,8},{10,9... | collective-permute-start | bytes 1966088 | tf_op jit(solution)/shard_map/ppermute | solution.py:61
  95.0 19.9 %collective-permute-start.10 = (bf16[128,2560]{1,0:T(8,128)(2,1)S(1)}, bf16[128,2560]{1,0:T(8,128)(2,1)S(1)}, u32[]{:S(2)}, u32[]{:S(2)}) collective-permute-start(bf16[128,2560]{1,0:T(8,128)(2,1)S(1)} %shard_map.62), channel_id=1, source_target_pairs={{0,1},{1,2},{2,3},{3,0},{4,5},{5,6},{6,7},{7,4},{8,11},{9,8},{10,9... | collective-permute-start | bytes 1966088 | tf_op jit(solution)/shard_map/ppermute | solution.py:61
  97.6 15.4 %collective-permute-start.14 = (bf16[128,1536]{1,0:T(8,128)(2,1)S(1)}, bf16[128,1536]{1,0:T(8,128)(2,1)S(1)}, u32[]{:S(2)}, u32[]{:S(2)}) collective-permute-start(bf16[128,1536]{1,0:T(8,128)(2,1)S(1)} %shard_map.65), channel_id=1, source_target_pairs={{0,1},{1,2},{2,3},{3,0},{4,5},{5,6},{6,7},{7,4},{8,11},{9,8},{10,9... | collective-permute-start | bytes 1179656 | tf_op jit(solution)/shard_map/ppermute | solution.py:61
  113.0 10.9 %collective-permute-start.15 = (bf16[128,1536]{1,0:T(8,128)(2,1)S(1)}, bf16[128,1536]{1,0:T(8,128)(2,1)S(1)}, u32[]{:S(2)}, u32[]{:S(2)}) collective-permute-start(bf16[128,1536]{1,0:T(8,128)(2,1)S(1)} %shard_map.66), channel_id=1, source_target_pairs={{0,1},{1,2},{2,3},{3,0},{4,5},{5,6},{6,7},{7,4},{8,11},{9,8},{10,9... | collective-permute-start | bytes 1179656 | tf_op jit(solution)/shard_map/ppermute | solution.py:61
  115.1 20.0 %collective-permute-start.11 = (bf16[128,2560]{1,0:T(8,128)(2,1)S(1)}, bf16[128,2560]{1,0:T(8,128)(2,1)S(1)}, u32[]{:S(2)}, u32[]{:S(2)}) collective-permute-start(bf16[128,2560]{1,0:T(8,128)(2,1)S(1)} %shard_map.63), channel_id=1, source_target_pairs={{0,1},{1,2},{2,3},{3,0},{4,5},{5,6},{6,7},{7,4},{8,11},{9,8},{10,9... | collective-permute-start | bytes 1966088 | tf_op jit(solution)/shard_map/ppermute | solution.py:61
  124.0 11.1 %collective-permute-start.16 = (bf16[128,1536]{1,0:T(8,128)(2,1)S(1)}, bf16[128,1536]{1,0:T(8,128)(2,1)S(1)}, u32[]{:S(2)}, u32[]{:S(2)}) collective-permute-start(bf16[128,1536]{1,0:T(8,128)(2,1)S(1)} %shard_map.67), channel_id=1, source_target_pairs={{0,1},{1,2},{2,3},{3,0},{4,5},{5,6},{6,7},{7,4},{8,11},{9,8},{10,9... | collective-permute-start | bytes 1179656 | tf_op jit(solution)/shard_map/ppermute | solution.py:61
